TPU v7x, 8 devices: a whole 2x2x1 slice. The times are simulated.
8 devices in a mesh: data: 8 (over z, y, x, core).
Axes of the slice: x: 2, y: 2, z: 1, core: 2. Of those that a mesh axis runs over, the one named last changes fastest.
Arguments:
- tokens: bfloat16 [4096, 1024], P('data')
- labels: int32 [3, 4096], P(None, 'data')
- w_one: bfloat16 [1024, 4096], replicated
- w_two: bfloat16 [4096, 1024], replicated
- adapter_a: bfloat16 [1024, 8], replicated
- adapter_b: bfloat16 [8, 4096], replicated
- task_heads: bfloat16 [3, 1024, 3], replicated
Outputs:
- output 1: float32 [3], replicated
- output 2: float32 [1024, 8], P('data')
- output 3: float32 [8, 4096], P(None, 'data')
All inputs are finite; a program needn't handle non-finite values.
Results may differ from a plain program's by a relative error of at most 0.00122422.
Values are sent between devices in bfloat16 or wider.
A program may use at most 1 GiB of HBM per device.

v0:
```python
import jax
import jax.numpy as jnp
from jax import lax
from jax.sharding import PartitionSpec as P

EG_STEPS = 20


def weight_solver(gram_mat):
    num_tasks = gram_mat.shape[0]
    eg_scale = jnp.trace(gram_mat) / num_tasks

    def eg_step(step_idx, weights):
        weights = weights * jnp.exp(-jnp.sum(gram_mat * weights[None, :], axis=1) / eg_scale)
        return weights / jnp.sum(weights)

    return lax.fori_loop(0, EG_STEPS, eg_step, jnp.full((num_tasks,), 1.0 / num_tasks, jnp.float32))


def task_grads(tokens, labels, w_one, w_two, adapter_a, adapter_b, task_heads):
    num_classes = task_heads.shape[2]
    low_rank = jnp.dot(tokens, adapter_a, preferred_element_type=jnp.float32).astype(jnp.bfloat16)
    pre_act = jnp.dot(tokens, w_one, preferred_element_type=jnp.float32) + jnp.dot(low_rank, adapter_b, preferred_element_type=jnp.float32)
    gelu_out, gelu_slope = jax.jvp(jax.nn.gelu, (pre_act,), (jnp.ones_like(pre_act),))
    hidden = gelu_out.astype(jnp.bfloat16)
    trunk_out = (tokens.astype(jnp.float32) + jnp.dot(hidden, w_two, preferred_element_type=jnp.float32)).astype(jnp.bfloat16)
    logits = jnp.einsum("bd,tdc->tbc", trunk_out, task_heads, preferred_element_type=jnp.float32)
    task_probs = jax.nn.softmax(logits, axis=-1)
    onehot = (labels[:, :, None] == jnp.arange(num_classes)[None, None, :]).astype(jnp.float32)
    logit_err = (task_probs - onehot).astype(jnp.bfloat16)
    d_trunk = jnp.einsum("tbc,tdc->tbd", logit_err, task_heads, preferred_element_type=jnp.float32).astype(jnp.bfloat16)
    d_hidden = jnp.einsum("tbd,fd->tbf", d_trunk, w_two, preferred_element_type=jnp.float32)
    d_pre = (d_hidden * gelu_slope[None]).astype(jnp.bfloat16)
    part_b = jnp.einsum("cs,ucg->usg", low_rank, d_pre, preferred_element_type=jnp.float32)
    d_low = jnp.einsum("tbf,rf->tbr", d_pre, adapter_b, preferred_element_type=jnp.float32).astype(jnp.bfloat16)
    part_a = jnp.einsum("bd,tbr->tdr", tokens, d_low, preferred_element_type=jnp.float32)
    return part_a, part_b


def solution(mesh):
    num_dev = mesh.shape["data"]

    def device_step(tokens, labels, w_one, w_two, adapter_a, adapter_b, task_heads):
        batch_total = tokens.shape[0] * num_dev
        part_a, part_b = task_grads(tokens, labels, w_one, w_two, adapter_a, adapter_b, task_heads)
        shard_a = lax.psum_scatter(part_a, "data", scatter_dimension=1, tiled=True) / batch_total
        shard_b = lax.psum_scatter(part_b, "data", scatter_dimension=2, tiled=True) / batch_total
        gram_part = jnp.einsum("tdr,sdr->ts", shard_a, shard_a, precision=lax.Precision.HIGHEST) + jnp.einsum("usg,tsg->ut", shard_b, shard_b, precision=lax.Precision.HIGHEST)
        gram_mat = lax.psum(gram_part, "data")
        task_weights = weight_solver(gram_mat)
        comb_a = jnp.sum(task_weights[:, None, None] * shard_a, axis=0)
        comb_b = jnp.sum(task_weights[:, None, None] * shard_b, axis=0)
        return task_weights, comb_a, comb_b

    return jax.shard_map(device_step, mesh=mesh, in_specs=(P("data", None), P(None, "data"), P(), P(), P(), P(), P()), out_specs=(P(), P("data", None), P(None, "data")), check_vma=False)
```

profile of v0, /device:TPU:0, one launch (start us, length us, event | category | flops | bytes accessed | tf_op | source)
XLA Modules:
  0.0 176.9 jit_solution(6640142889632531747)
XLA Ops:
  7.2 1.6 convolution_convert_fusion.1
  8.8 7.4 %fusion.39 = f32[512,4096]{1,0:T(8,128)S(1)} fusion(bf16[512,1024]{1,0:T(8,128)(2,1)} %param.9, bf16[1024,4096]{1,0:T(8,128)(2,1)} %param.11), kind=kOutput, calls=%fused_computation.59 | convolution fusion | flops 4294967296 | bytes 17825792 | tf_op jit(solution)/shard_map/dot_general | solution.py:23
  16.2 7.2 %fusion.10 = (f32[512,4096]{1,0:T(8,128)}, f32[512,4096]{1,0:T(8,128)S(1)}) fusion(f32[512,4096]{1,0:T(8,128)S(1)} %fusion.39, bf16[512,8]{0,1:T(8,128)(2,1)S(1)} %convolution_convert_fusion.1, bf16[8,4096]{1,0:T(8,128)(2,1)S(1)} %copy-done), kind=kOutput, calls=%fused_computation.17 | convolution fusion | flops 69206016 | bytes 25239552 | tf_op jit(solution)/shard_map/dot_general | solution.py:23
  23.5 5.2 %fusion.16 = bf16[512,1024,1]{1,0,2:T(8,128)(2,1)S(1)} fusion(bf16[4096,1024]{1,0:T(8,128)(2,1)S(1)} %bitcast.42, f32[512,4096]{1,0:T(8,128)S(1)} %get-tuple-element.52, bf16[512,1024]{1,0:T(8,128)(2,1)S(1)} %copy-done.1), kind=kOutput, calls=%fused_computation.26 | convolution fusion | flops 4315414528 | bytes 18874368 | tf_op jit(solution)/shard_map/dot_general | solution.py:26
  28.8 0.4 fusion.38
  29.2 20.3 %multiply_convert_fusion = bf16[3,512,4096]{2,1,0:T(8,128)(2,1)} fusion(f32[512,4096]{1,0:T(8,128)} %get-tuple-element.51, bf16[4096,1024]{1,0:T(8,128)(2,1)} %param.12, bf16[3,1024,3]{1,2,0:T(4,128)(2,1)S(1)} %copy-done.2, f32[3,512,3]{1,2,0:T(4,128)S(1)} %get-tuple-element.54, s32[3,512]{1,0:T(4,128)S(1)} %copy-done.4, f32[3,512]{1,0:T(4,128)S(1)} %get-tuple-element.53), kind=kOutput, calls=%fused_computation.5 | convolution fusion | flops 12908517376 | bytes 29409280 | tf_op jit(solution)/shard_map/tbd,fd->tbf/dot_general | solution.py:32
  49.5 8.8 %convolution_bitcast_fusion.1 = f32[3,1024,8]{1,2,0:T(8,128)} fusion(bf16[3,512,4096]{2,1,0:T(8,128)(2,1)} %multiply_convert_fusion, bf16[512,1024]{1,0:T(8,128)(2,1)S(1)} %copy-done.1, bf16[8,4096]{1,0:T(8,128)(2,1)S(1)} %copy-done), kind=kOutput, calls=%fused_computation.27 | convolution fusion | flops 125841408 | bytes 13795328 | tf_op jit(solution)/shard_map/bd,tbr->tdr/dot_general | solution.py:36
  58.3 7.1 %convolution_bitcast_fusion = f32[3,8,4096]{2,1,0:T(8,128)} fusion(bf16[3,512,4096]{2,1,0:T(8,128)(2,1)} %multiply_convert_fusion, bf16[512,8]{0,1:T(8,128)(2,1)S(1)} %convolution_convert_fusion.1), kind=kOutput, calls=%fused_computation.21 | convolution fusion | flops 100663296 | bytes 12984320 | tf_op jit(solution)/shard_map/cs,ucg->usg/dot_general | solution.py:34
  65.5 19.9 %reduce-scatter.3.cloned.1.call-done = f32[3,128,8]{1,2,0:T(8,128)} async-done(((f32[3,1024,8]{1,2,0:T(8,128)}), f32[3,128,8]{1,2,0:T(8,128)}) %reduce-scatter.3.cloned.1.call-update) | async-done | bytes 12304 | tf_op jit(solution)/shard_map/reduce_scatter | solution.py:46
  85.4 0.7 broadcast_multiply_fusion.1
  86.1 27.8 %reduce-scatter.5.cloned.1.call-done = f32[3,8,512]{2,1,0:T(8,128)} async-done(((f32[3,8,4096]{2,1,0:T(8,128)}), f32[3,8,512]{2,1,0:T(8,128)}) %reduce-scatter.5.cloned.1.call-update) | async-done | bytes 49168 | tf_op jit(solution)/shard_map/reduce_scatter | solution.py:47
  113.9 0.8 broadcast_multiply_fusion
  114.7 0.4 convolution_bitcast_fusion.3
  115.1 0.2 fusion.19
  115.3 22.3 %psum.7 = f32[3,3]{1,0:T(4,128)S(1)} all-reduce(f32[3,3]{1,0:T(4,128)S(1)} %fusion.19), channel_id=1, replica_groups=mesh['data'=8] {'data'}, use_global_device_ids=true, to_apply=%region_4.0 | all-reduce | flops 9 | bytes 72 | tf_op jit(solution)/shard_map/psum | solution.py:49
  137.6 0.6 select_reduce_fusion
  138.8 28.4 %while.11 = (s32[]{:T(128)}, f32[3]{0:T(128)S(1)}, f32[3,3]{1,0:T(4,128)S(1)}, f32[]{:T(128)}, s32[]{:T(128)}, /*index=5*/s32[]{:T(128)}) while((s32[]{:T(128)}, f32[3]{0:T(128)S(1)}, f32[3,3]{1,0:T(4,128)S(1)}, f32[]{:T(128)}, s32[]{:T(128)}, /*index=5*/s32[]{:T(128)}) %tuple.31), condition=%wide.region_9.10_spmd.clone, body=%wide.region_6.9_spmd.clone.sunk | while | flops 38 | bytes 236 | solution.py:17
  138.9 0.6 fusion.53
  139.6 0.6 broadcast_divide_fusion.2
  140.3 0.1 multiply_reduce_fusion.4
  140.4 0.6 fusion.53
  141.0 0.6 broadcast_divide_fusion.2
  141.8 0.6 fusion.53
  142.4 0.6 broadcast_divide_fusion.2
  143.2 0.6 fusion.53
  143.8 0.6 broadcast_divide_fusion.2
  144.5 0.1 multiply_reduce_fusion.4
  144.6 0.6 fusion.53
  145.2 0.6 broadcast_divide_fusion.2
  146.0 0.6 fusion.53
  146.7 0.6 broadcast_divide_fusion.2
  147.5 0.6 fusion.53
  148.1 0.6 broadcast_divide_fusion.2
  148.8 0.1 multiply_reduce_fusion.4
  148.9 0.6 fusion.53
  149.5 0.6 broadcast_divide_fusion.2
  150.2 0.1 multiply_reduce_fusion.4
  150.3 0.6 fusion.53
  150.9 0.6 broadcast_divide_fusion.2
  151.7 0.6 fusion.53
  152.3 0.6 broadcast_divide_fusion.2
  153.0 0.1 multiply_reduce_fusion.4
  153.1 0.6 fusion.53
  153.8 0.6 broadcast_divide_fusion.2
  154.6 0.6 fusion.53
  155.2 0.6 broadcast_divide_fusion.2
  156.0 0.6 fusion.53
  156.6 0.6 broadcast_divide_fusion.2
  157.4 0.6 fusion.53
  158.0 0.6 broadcast_divide_fusion.2
  158.8 0.6 fusion.53
  159.4 0.6 broadcast_divide_fusion.2
  160.2 0.6 fusion.53
  160.9 0.6 broadcast_divide_fusion.2
  161.7 0.6 fusion.53
  162.3 0.6 broadcast_divide_fusion.2
  163.1 0.6 fusion.53
  163.7 0.6 broadcast_divide_fusion.2
  164.5 0.6 fusion.53
  165.1 0.6 broadcast_divide_fusion.2
  165.9 0.6 fusion.53
  166.5 0.6 broadcast_divide_fusion.2
  167.2 1.5 multiply_reduce_fusion.1
  168.7 1.4 multiply_reduce_fusion.2
  (56 shorter events, 2.0 us)
Async XLA Ops:
  7.2 9.0 %copy-start = (bf16[8,4096]{1,0:T(8,128)(2,1)S(1)}, bf16[8,4096]{1,0:T(8,128)(2,1)}, u32[]{:S(2)}) copy-start(bf16[8,4096]{1,0:T(8,128)(2,1)} %param.14) | copy-start | bytes 196612
  7.2 78.2 %reduce-scatter.3.cloned.1.call-start = ((), (), s32[]{:S(2)}) async-start(), calls=%async_computation.2 | async-start | bytes 110592 | tf_op jit(solution)/shard_map/reduce_scatter | solution.py:46
  8.8 14.6 %slice-start = ((s8[8388608]{0:T(1024)(128)(4,1)}), s8[4194304]{0:T(1024)(128)(4,1)S(1)}, s32[]{:S(2)}) async-start(s8[8388608]{0:T(1024)(128)(4,1)} %bitcast.41), calls=%async_computation.4 | async-start | bytes 8388608
  16.2 7.3 %copy-start.1 = (bf16[512,1024]{1,0:T(8,128)(2,1)S(1)}, bf16[512,1024]{1,0:T(8,128)(2,1)}, u32[]{:S(2)}) copy-start(bf16[512,1024]{1,0:T(8,128)(2,1)} %param.9) | copy-start | bytes 3145732
  16.2 7.3 %slice-start.1 = ((s8[8388608]{0:T(1024)(128)(4,1)}), s8[4194304]{0:T(1024)(128)(4,1)S(1)}, s32[]{:S(2)}) async-start(s8[8388608]{0:T(1024)(128)(4,1)} %bitcast.41), calls=%async_computation.5 | async-start | bytes 8388608
  23.5 5.3 %copy-start.2 = (bf16[3,1024,3]{1,2,0:T(4,128)(2,1)S(1)}, bf16[3,1024,3]{1,2,0:T(4,128)(2,1)}, u32[]{:S(2)}) copy-start(bf16[3,1024,3]{1,2,0:T(4,128)(2,1)} %param.15) | copy-start | bytes 55300
  23.5 5.7 %copy-start.4 = (s32[3,512]{1,0:T(4,128)S(1)}, s32[3,512]{1,0:T(4,128)}, u32[]{:S(2)}) copy-start(s32[3,512]{1,0:T(4,128)} %param.10) | copy-start | bytes 18436
  58.3 55.6 %reduce-scatter.5.cloned.1.call-start = ((), (), s32[]{:S(2)}) async-start(), calls=%async_computation.3 | async-start | bytes 442368 | tf_op jit(solution)/shard_map/reduce_scatter | solution.py:47
  167.2 2.9 %copy-start.3 = (f32[3]{0:T(128)}, f32[3]{0:T(128)S(1)}, u32[]{:S(2)}) copy-start(f32[3]{0:T(128)S(1)} %get-tuple-element.22) | copy-start | bytes 40
Sparse Core Ops, SparseCore 0:
  58.4 26.8 reduce-scatter.2
  88.3 25.5 reduce-scatter.4
where the time goes:
time: 178 us; the launch traced here: 177 us
  matrix products  58.6 us (33%)
  waiting for transfers between devices  47.7 us (27%)
  other arithmetic  32.7 us (18%)
  blocking collectives  22.3 us (13%)
  between operations  14.8 us (8%)
    reduce_scatter x1, waiting for transfers between devices, device_step(): lax.psum_scatter(part_b, 'data', scatter_dimension=2, tiled=True)  27.8 us
    psum x1, blocking collectives, device_step(): gram_mat = lax.psum(gram_part, 'data')  22.3 us
    dot_general x1, matrix products, task_grads(): jnp.einsum('tbd,fd->tbf', d_trunk, w_two, preferred_element_type=jnp.floa...  20.3 us
    reduce_scatter x1, waiting for transfers between devices, device_step(): lax.psum_scatter(part_a, 'data', scatter_dimension=1, tiled=True)  19.9 us
    div x20, other arithmetic, eg_step(): return weights / jnp.sum(weights)  13 us
    reduce_sum x20, other arithmetic, eg_step(): return weights / jnp.sum(weights)  12.4 us
    dot_general x1, matrix products, task_grads(): jnp.einsum('bd,tbr->tdr', tokens, d_low, preferred_element_type=jnp.float32)  8.76 us
    dot_general x1, matrix products, task_grads(): jnp.dot(tokens, w_one, preferred_element_type=jnp.float32)  7.36 us
  transfers between devices with their start and end apart: 2, of which 2 were waited for; matrix products, arithmetic and copies ran while one was open for 4% of the time, Pallas kernels for 0%

commit v1 on v0

v1 whole, which is shorter than its diff:
```python
import functools

import jax
import jax.numpy as jnp
import numpy as np
from jax import lax
from jax.experimental import pallas as pl
from jax.experimental.pallas import tpu as pltpu
from jax.sharding import PartitionSpec as P

EG_STEPS = 20
MESH = pl.DeviceIdType.MESH
F32, BF16 = jnp.float32, jnp.bfloat16
GELU_C = float(np.sqrt(2.0 / np.pi))
GELU_A = 0.044715
NT = (((1,), (1,)), ((), ()))


def dot(lhs, rhs):
    return jnp.dot(lhs, rhs, preferred_element_type=F32)


def dot_nt(lhs, rhs):
    return lax.dot_general(lhs, rhs, NT, preferred_element_type=F32)


def fused_kernel(ndev, batch_total, x_hbm, lab_hbm, w1_hbm, w2_hbm, at_hbm, bm_hbm, ht_hbm,
                 alpha_ref, ga_ref, gb_ref,
                 xs, w1s, w2s, ats, bms, hts_in, labs, uts, us, p_a, p_b, h_a, h_b, slope, zacc, zs,
                 hfs, hrow, hcat, dzs, dp_a, dp_b, dlacc, gbs, gbr, gas, gar, ms, mr,
                 w1sem, w2sem, insem, gb_ss, gb_rs, ga_ss, ga_rs, m_ss, m_rs):
    tok = xs.shape[0]
    dff = w2_hbm.shape[0]
    fb = dff // ndev
    rank = ats.shape[0]
    tasks = hts_in.shape[0]
    ncls = hts_in.shape[1]
    dm = xs.shape[1]
    own = dm // ndev
    me = lax.axis_index("data")

    barrier = pltpu.get_barrier_semaphore()
    for off in range(1, ndev):
        pl.semaphore_signal(barrier, inc=1, device_id=(lax.rem(me + off, ndev),), device_id_type=MESH)

    def small(i):
        pairs = [(at_hbm, ats), (x_hbm, xs), (bm_hbm, bms), (ht_hbm, hts_in), (lab_hbm, labs)]
        return pltpu.make_async_copy(pairs[i][0], pairs[i][1], insem.at[i])

    def w1_copy(j):
        return pltpu.make_async_copy(w1_hbm.at[:, pl.ds(pl.multiple_of(j * fb, fb), fb)], w1s.at[j], w1sem.at[j])

    def w2_copy(j):
        return pltpu.make_async_copy(w2_hbm.at[pl.ds(pl.multiple_of(j * fb, fb), fb), :], w2s.at[j], w2sem.at[j])

    for i in range(3):
        small(i).start()
    w1_copy(0).start()
    w1_copy(1).start()
    w2_copy(0).start()
    small(3).start()
    small(4).start()
    for j in range(2, ndev):
        w1_copy(j).start()
        w2_copy(j - 1).start()
    w2_copy(ndev - 1).start()

    small(0).wait()
    small(1).wait()
    ut = dot_nt(ats[...], xs[...])
    uts[...] = ut.astype(BF16)
    us[...] = ut.T.astype(BF16)
    small(2).wait()
    zacc[...] = jnp.zeros_like(zacc)
    dlacc[...] = jnp.zeros_like(dlacc)
    hfs[...] = jnp.zeros_like(hfs)

    def block_of(ref, j):
        return ref[:, pl.ds(pl.multiple_of(j * fb, fb), fb)]

    def fwd_in(j, p_ref):
        w1_copy(j).wait()
        p_ref[...] = dot(xs[...], w1s[j]) + dot(us[...], block_of(bms, j))

    def fwd_act(j, p_ref, h_ref):
        x = p_ref[...]
        x2 = x * x
        t = jnp.tanh(x * (GELU_C + (GELU_C * GELU_A) * x2))
        cdf = 0.5 + 0.5 * t
        h_ref[...] = (x * cdf).astype(BF16)
        w = cdf * (1.0 - cdf)
        slope[j] = cdf + x * (w * (2.0 * GELU_C + (6.0 * GELU_C * GELU_A) * x2))

    def fwd_out(j, h_ref):
        w2_copy(j).wait()
        zacc[...] += dot(h_ref[...], w2s[j])

    ps, hs = (p_a, p_b), (h_a, h_b)
    fwd_in(0, p_a)
    fwd_in(1, p_b)
    fwd_act(0, p_a, h_a)

    def fwd_pair(i, carry):
        for k in range(2):
            j = 2 * i + k
            fwd_in(j + 2, ps[k])
            fwd_act(j + 1, ps[1 - k], hs[1 - k])
            fwd_out(j, hs[k])
        return carry

    lax.fori_loop(0, (ndev - 2) // 2, fwd_pair, 0)
    fwd_act(ndev - 1, p_b, h_b)
    fwd_out(ndev - 2, h_a)
    fwd_out(ndev - 1, h_b)

    small(3).wait()
    small(4).wait()
    for t in range(tasks):
        head = hts_in[t].astype(F32)
        hfs[8 * t:8 * t + ncls, dm * t:dm * (t + 1)] = head
    hcat[...] = hfs[...].astype(BF16)
    rows = hfs[:, 0:dm]
    for t in range(1, tasks):
        rows = rows + hfs[:, dm * t:dm * (t + 1)]
    hrow[...] = rows.astype(BF16)

    zs[...] = (xs[...].astype(F32) + zacc[...]).astype(BF16)
    logits = dot_nt(hrow[...], zs[...])
    cls = lax.broadcasted_iota(jnp.int32, (8, tok), 0)
    errs = []
    for t in range(tasks):
        lg = jnp.where(cls < ncls, logits[8 * t:8 * t + 8], -jnp.inf)
        e = jnp.exp(lg - jnp.max(lg, axis=0, keepdims=True))
        prob = e / jnp.sum(e, axis=0, keepdims=True)
        errs.append(prob - (cls == labs[t:t + 1, :]).astype(F32))
    errs.append(jnp.zeros((8, tok), F32))
    err_t = jnp.concatenate(errs, axis=0).T.astype(BF16)
    for t in range(tasks):
        dzs[t] = dot(err_t, hcat[:, dm * t:dm * (t + 1)]).astype(BF16)

    pl.semaphore_wait(barrier, ndev - 1)

    def blk(s):
        return lax.rem(me + 1 + s, ndev)

    def bwd_a(s, dp_ref):
        b = blk(s)
        for t in range(tasks):
            dp_ref[t] = (dot_nt(dzs[t], w2s[b]) * slope[b]).astype(BF16)

    def bwd_b(s, dp_ref):
        b = blk(s)
        bm = block_of(bms, b)
        for t in range(tasks):
            gbs[s, 8 * t:8 * t + 8] = dot(uts[...], dp_ref[t])
            dlacc[8 * t:8 * t + 8] += dot_nt(bm, dp_ref[t])

    def gb_send(s):
        return pltpu.make_async_remote_copy(src_ref=gbs.at[s], dst_ref=gbr.at[s], send_sem=gb_ss.at[s], recv_sem=gb_rs.at[s],
                                            device_id=(blk(s),), device_id_type=MESH)

    dps = (dp_a, dp_b)
    bwd_a(0, dp_a)

    def bwd_pair(i, carry):
        for k in range(2):
            s = 2 * i + k
            bwd_a(s + 1, dps[1 - k])
            bwd_b(s, dps[k])
            gb_send(s).start()
        return carry

    lax.fori_loop(0, (ndev - 2) // 2, bwd_pair, 0)
    bwd_a(ndev - 1, dp_b)
    bwd_b(ndev - 2, dp_a)
    gb_send(ndev - 2).start()
    bwd_b(ndev - 1, dp_b)

    ga_t = dot(dlacc[...].astype(BF16), xs[...])
    for k in range(ndev):
        gas[k] = ga_t[:8 * tasks, own * k:own * (k + 1)]

    def ga_send(off):
        peer = lax.rem(me + off, ndev)
        return pltpu.make_async_remote_copy(src_ref=gas.at[peer], dst_ref=gar.at[off - 1], send_sem=ga_ss.at[off - 1], recv_sem=ga_rs.at[off - 1],
                                            device_id=(peer,), device_id_type=MESH)

    for off in range(1, ndev):
        ga_send(off).start()

    gb_sum = gbs[ndev - 1]
    for s in range(ndev - 1):
        gb_send(s).wait_recv()
        gb_sum = gb_sum + gbr[s]
    gb_sum = gb_sum * (1.0 / batch_total)

    pairs = [(t, s) for t in range(tasks) for s in range(t, tasks)]
    gram_b = []
    for t, s in pairs:
        prod = gb_sum[8 * t:8 * t + 8] * gb_sum[8 * s:8 * s + 8]
        tot = prod[:, 0:128]
        for k in range(1, fb // 128):
            tot = tot + prod[:, 128 * k:128 * (k + 1)]
        gram_b.append(tot)

    ga_sum = gas[me]
    for off in range(1, ndev):
        ga_send(off).wait_recv()
        ga_sum = ga_sum + gar[off - 1]
    ga_sum = ga_sum * (1.0 / batch_total)

    ms[...] = jnp.zeros_like(ms)
    for p, (t, s) in enumerate(pairs):
        prod = ga_sum[8 * t:8 * t + 8] * ga_sum[8 * s:8 * s + 8] + gram_b[p]
        ms[p:p + 1, :] = jnp.sum(prod, axis=0, keepdims=True)

    def m_send(off):
        peer = lax.rem(me + off, ndev)
        return pltpu.make_async_remote_copy(src_ref=ms, dst_ref=mr.at[me], send_sem=m_ss.at[off - 1], recv_sem=m_rs.at[off - 1],
                                            device_id=(peer,), device_id_type=MESH)

    for off in range(1, ndev):
        m_send(off).start()
    mr[me] = ms[...]
    for off in range(1, ndev):
        m_send(off).wait_recv()
    m_tot = mr[0]
    for k in range(1, ndev):
        m_tot = m_tot + mr[k]
    m_tot = jnp.sum(m_tot, axis=1, keepdims=True)
    m_all = jnp.broadcast_to(m_tot, (8, 128))

    gram = {}
    for p, (t, s) in enumerate(pairs):
        gram[t, s] = gram[s, t] = jnp.broadcast_to(m_all[p:p + 1, :], (8, 128))
    trace = gram[0, 0]
    for t in range(1, tasks):
        trace = trace + gram[t, t]
    scale = trace / tasks
    gram = {key: val / scale for key, val in gram.items() if key[0] <= key[1]}

    def eg_step(_, wts):
        new = []
        for t in range(tasks):
            acc = gram[min(t, 0), max(t, 0)] * wts[0]
            for s in range(1, tasks):
                acc = acc + gram[min(t, s), max(t, s)] * wts[s]
            new.append(wts[t] * jnp.exp(-acc))
        tot = new[0]
        for t in range(1, tasks):
            tot = tot + new[t]
        inv = 1.0 / tot
        return tuple(w * inv for w in new)

    wts = lax.fori_loop(0, EG_STEPS, eg_step, tuple(jnp.full((8, 128), 1.0 / tasks, F32) for _ in range(tasks)))

    ga = wts[0] * ga_sum[0:8]
    for t in range(1, tasks):
        ga = ga + wts[t] * ga_sum[8 * t:8 * t + 8]
    ga_ref[...] = ga
    for k in range(fb // 128):
        cols = slice(128 * k, 128 * (k + 1))
        gb = wts[0] * gb_sum[0:8, cols]
        for t in range(1, tasks):
            gb = gb + wts[t] * gb_sum[8 * t:8 * t + 8, cols]
        gb_ref[:, cols] = gb
    lane = lax.broadcasted_iota(jnp.int32, (8, 128), 1)
    alpha = wts[tasks - 1]
    for t in range(tasks - 1):
        alpha = jnp.where(lane == t, wts[t], alpha)
    alpha_ref[...] = alpha[0:1, 0:tasks]

    for s in range(ndev - 1):
        gb_send(s).wait_send()
    for off in range(1, ndev):
        ga_send(off).wait_send()
        m_send(off).wait_send()


def solution(mesh):
    num_dev = mesh.shape["data"]

    def device_step(tokens, labels, w_one, w_two, adapter_a, adapter_b, task_heads):
        tok, dm = tokens.shape
        rank, dff = adapter_b.shape
        tasks, _, ncls = task_heads.shape
        fb = dff // num_dev
        own = dm // num_dev
        prow = 8 * tasks + 8
        dma = pltpu.SemaphoreType.DMA
        hbm = pl.BlockSpec(memory_space=pl.ANY)
        vmem = pl.BlockSpec(memory_space=pltpu.VMEM)
        alpha, ga, gb = pl.pallas_call(
            functools.partial(fused_kernel, num_dev, float(tok * num_dev)),
            name="fused_grads",
            out_shape=(jax.ShapeDtypeStruct((1, tasks), F32), jax.ShapeDtypeStruct((rank, own), F32), jax.ShapeDtypeStruct((rank, fb), F32)),
            in_specs=[hbm] * 7,
            out_specs=(vmem, vmem, vmem),
            scratch_shapes=[
                pltpu.VMEM((tok, dm), BF16),
                pltpu.VMEM((num_dev, dm, fb), BF16),
                pltpu.VMEM((num_dev, fb, dm), BF16),
                pltpu.VMEM((rank, dm), BF16),
                pltpu.VMEM((rank, dff), BF16),
                pltpu.VMEM((tasks, ncls, dm), BF16),
                pltpu.VMEM((tasks, tok), jnp.int32),
                pltpu.VMEM((rank, tok), BF16),
                pltpu.VMEM((tok, rank), BF16),
                pltpu.VMEM((tok, fb), F32),
                pltpu.VMEM((tok, fb), F32),
                pltpu.VMEM((tok, fb), BF16),
                pltpu.VMEM((tok, fb), BF16),
                pltpu.VMEM((num_dev, tok, fb), F32),
                pltpu.VMEM((tok, dm), F32),
                pltpu.VMEM((tok, dm), BF16),
                pltpu.VMEM((prow, tasks * dm), F32),
                pltpu.VMEM((prow, dm), BF16),
                pltpu.VMEM((prow, tasks * dm), BF16),
                pltpu.VMEM((tasks, tok, dm), BF16),
                pltpu.VMEM((tasks, tok, fb), BF16),
                pltpu.VMEM((tasks, tok, fb), BF16),
                pltpu.VMEM((prow, tok), F32),
                pltpu.VMEM((num_dev, 8 * tasks, fb), F32),
                pltpu.VMEM((num_dev - 1, 8 * tasks, fb), F32),
                pltpu.VMEM((num_dev, 8 * tasks, own), F32),
                pltpu.VMEM((num_dev - 1, 8 * tasks, own), F32),
                pltpu.VMEM((8, 128), F32),
                pltpu.VMEM((num_dev, 8, 128), F32),
                dma((num_dev,)),
                dma((num_dev,)),
                dma((5,)),
                dma((num_dev - 1,)),
                dma((num_dev - 1,)),
                dma((num_dev - 1,)),
                dma((num_dev - 1,)),
                dma((num_dev - 1,)),
                dma((num_dev - 1,)),
            ],
            compiler_params=pltpu.CompilerParams(collective_id=0, has_side_effects=True, vmem_limit_bytes=60 * 1024 * 1024),
        )(tokens, labels, w_one, w_two, adapter_a.T, adapter_b, jnp.transpose(task_heads, (0, 2, 1)))
        return alpha.reshape(tasks), ga.T, gb

    return jax.shard_map(device_step, mesh=mesh, in_specs=(P("data", None), P(None, "data"), P(), P(), P(), P(), P()), out_specs=(P(), P("data", None), P(None, "data")), check_vma=False)
```

time: 178 us -> 60 us (0.34)
  matrix products: 58.6 us -> 0 us
  Pallas kernels: 0 us -> 55.3 us
  waiting for transfers between devices: 47.7 us -> 0 us
  other arithmetic: 32.7 us -> 0 us
  blocking collectives: 22.3 us -> 0 us
  between operations: 14.8 us -> 0.64 us
  local copies, waits for them, and re-layouts: 0.05 us -> 3.76 us
    dot_general x9 -> x0, matrix products: 58.2 us -> none  [the longest x1 20.3 us: task_grads(): jnp.einsum('tbd,fd->tbf', d_trunk, w_two, preferred_element_type=jnp.floa...]
    pallas_call x0 -> x1, Pallas kernels: none -> 55.3 us  [device_step(): pl.pallas_call(functools.partial(fused_kernel, num_dev, float(tok * num_d...]
    reduce_scatter x2 -> x0, waiting for transfers between devices: 47.7 us -> none  [the longest x1 27.8 us: device_step(): lax.psum_scatter(part_b, 'data', scatter_dimension=2, tiled=True)]
    psum x1 -> x0, blocking collectives: 22.3 us -> none  [device_step(): gram_mat = lax.psum(gram_part, 'data')]
    reduce_sum x43 -> x0, other arithmetic: 18.1 us -> none  [the longest x20 12.4 us: eg_step(): return weights / jnp.sum(weights)]
    div x22 -> x0, other arithmetic: 14.5 us -> none  [the longest x20 13 us: eg_step(): return weights / jnp.sum(weights)]
    unnamed x14 -> x3, local copies, waits for them, and re-layouts: 0.05 us -> 3.76 us
  transfers between devices with their start and end apart: 2 -> 0, of which waited for: 2 -> 0; matrix products, arithmetic and copies ran while one was open for 4% -> 0% of each run, Pallas kernels for 0% -> 0%
where the time goes in v1:
time: 60 us; the launch traced here: 59.7 us
  Pallas kernels  55.3 us (92%)
  local copies, waits for them, and re-layouts  3.76 us (6%)
  between operations  0.64 us (1%)
    pallas_call x1, Pallas kernels, device_step(): pl.pallas_call(functools.partial(fused_kernel, num_dev, float(tok * num_d...  55.3 us
    unnamed x3, local copies, waits for them, and re-layouts  3.76 us

profile of v1, /device:TPU:0, one launch (start us, length us, event | category | flops | bytes accessed | tf_op | source)
XLA Modules:
  0.0 59.7 jit_solution(7413123702788553072)
XLA Ops:
  0.6 55.3 %fused_grads.1 = (f32[1,3]{1,0:T(1,128)}, f32[8,128]{1,0:T(8,128)}, f32[8,512]{1,0:T(8,128)}) custom-call(bf16[512,1024]{1,0:T(8,128)(2,1)} %x_hbm.1, s32[3,512]{1,0:T(4,128)} %lab_hbm.1, bf16[1024,4096]{1,0:T(8,128)(2,1)} %w1_hbm.1, bf16[4096,1024]{1,0:T(8,128)(2,1)} %w2_hbm.1, bf16[8,1024]{1,0:T(8,128)(2,1)} %bitcast.5, bf16[8,4096]{1,0:T(8,128)(2,1)} %bm_hbm.1, ...), custom_call_target="tpu_custom_call" | custom-call | tf_op jit(solution)/shard_map/fused_grads/pallas_call | solution.py:293
  56.0 1.2 %copy.13 = f32[3]{0:T(128)} copy(f32[3]{0:T(128)} %bitcast.7) | data formatting | bytes 24
  57.2 1.3 %copy.14 = f32[128,8]{0,1:T(8,128)} copy(f32[128,8]{0,1:T(8,128)} %bitcast.6) | data formatting | bytes 8192
  58.4 1.3 %copy.15 = f32[8,512]{1,0:T(8,128)} copy(f32[8,512]{1,0:T(8,128)} %get-tuple-element.14) | data formatting | bytes 32768

commit v2 on v1

--- a/solution.py
+++ b/solution.py
@@ -25,8 +25,8 @@
 
 
 def fused_kernel(ndev, batch_total, x_hbm, lab_hbm, w1_hbm, w2_hbm, at_hbm, bm_hbm, ht_hbm,
-                 alpha_ref, ga_ref, gb_ref,
-                 xs, w1s, w2s, ats, bms, hts_in, labs, uts, us, p_a, p_b, h_a, h_b, slope, zacc, zs,
+                 m_out, ga_out, gb_out,
+                 xs, w1s, w2s, ats, bms, hts_in, labs, uts, us, p_a, p_b, h_a, h_b, slope, zacc,
                  hfs, hrow, hcat, dzs, dp_a, dp_b, dlacc, gbs, gbr, gas, gar, ms, mr,
                  w1sem, w2sem, insem, gb_ss, gb_rs, ga_ss, ga_rs, m_ss, m_rs):
     tok = xs.shape[0]
@@ -53,17 +53,29 @@
     def w2_copy(j):
         return pltpu.make_async_copy(w2_hbm.at[pl.ds(pl.multiple_of(j * fb, fb), fb), :], w2s.at[j], w2sem.at[j])
 
-    for i in range(3):
+    for i in (3, 0, 1):
         small(i).start()
     w1_copy(0).start()
     w1_copy(1).start()
+    small(2).start()
+    small(4).start()
     w2_copy(0).start()
-    small(3).start()
-    small(4).start()
     for j in range(2, ndev):
         w1_copy(j).start()
         w2_copy(j - 1).start()
     w2_copy(ndev - 1).start()
+
+    zacc[...] = jnp.zeros_like(zacc)
+    dlacc[...] = jnp.zeros_like(dlacc)
+    hfs[...] = jnp.zeros_like(hfs)
+    small(3).wait()
+    for t in range(tasks):
+        hfs[8 * t:8 * t + ncls, dm * t:dm * (t + 1)] = hts_in[t].astype(F32)
+    hcat[...] = hfs[...].astype(BF16)
+    head_rows = hfs[:, 0:dm]
+    for t in range(1, tasks):
+        head_rows = head_rows + hfs[:, dm * t:dm * (t + 1)]
+    hrow[...] = head_rows.astype(BF16)
 
     small(0).wait()
     small(1).wait()
@@ -71,89 +83,104 @@
     uts[...] = ut.astype(BF16)
     us[...] = ut.T.astype(BF16)
     small(2).wait()
-    zacc[...] = jnp.zeros_like(zacc)
-    dlacc[...] = jnp.zeros_like(dlacc)
-    hfs[...] = jnp.zeros_like(hfs)
+    small(4).wait()
+    w1_copy(0).wait()
+    w1_copy(1).wait()
 
     def block_of(ref, j):
         return ref[:, pl.ds(pl.multiple_of(j * fb, fb), fb)]
 
-    def fwd_in(j, p_ref):
-        w1_copy(j).wait()
-        p_ref[...] = dot(xs[...], w1s[j]) + dot(us[...], block_of(bms, j))
-
-    def fwd_act(j, p_ref, h_ref):
-        x = p_ref[...]
+    half, quarter = tok // 2, tok // 4
+
+    def fwd_in(j, p_ref, i):
+        rows = slice(half * i, half * (i + 1))
+        p_ref[rows] = dot(xs[rows], w1s[j]) + dot(us[rows], block_of(bms, j))
+
+    def fwd_act(j, p_ref, h_ref, i):
+        rows = slice(quarter * i, quarter * (i + 1))
+        x = p_ref[rows]
         x2 = x * x
         t = jnp.tanh(x * (GELU_C + (GELU_C * GELU_A) * x2))
         cdf = 0.5 + 0.5 * t
-        h_ref[...] = (x * cdf).astype(BF16)
+        h_ref[rows] = (x * cdf).astype(BF16)
         w = cdf * (1.0 - cdf)
-        slope[j] = cdf + x * (w * (2.0 * GELU_C + (6.0 * GELU_C * GELU_A) * x2))
-
-    def fwd_out(j, h_ref):
-        w2_copy(j).wait()
-        zacc[...] += dot(h_ref[...], w2s[j])
+        slope[j, rows] = cdf + x * (w * (2.0 * GELU_C + (6.0 * GELU_C * GELU_A) * x2))
+
+    def fwd_out(j, h_ref, i):
+        rows = slice(half * i, half * (i + 1))
+        zacc[rows] += dot(h_ref[rows], w2s[j])
 
     ps, hs = (p_a, p_b), (h_a, h_b)
-    fwd_in(0, p_a)
-    fwd_in(1, p_b)
-    fwd_act(0, p_a, h_a)
+    for i in range(2):
+        fwd_in(0, p_a, i)
+    for i in range(2):
+        fwd_in(1, p_b, i)
+        fwd_act(0, p_a, h_a, 2 * i)
+        fwd_act(0, p_a, h_a, 2 * i + 1)
 
     def fwd_pair(i, carry):
         for k in range(2):
+            w1_copy(2 * i + k + 2).wait()
+            w2_copy(2 * i + k).wait()
+        for k in range(2):
             j = 2 * i + k
-            fwd_in(j + 2, ps[k])
-            fwd_act(j + 1, ps[1 - k], hs[1 - k])
-            fwd_out(j, hs[k])
+            for q in range(4):
+                if q < 2:
+                    fwd_in(j + 2, ps[k], q)
+                else:
+                    fwd_out(j, hs[k], q - 2)
+                fwd_act(j + 1, ps[1 - k], hs[1 - k], q)
         return carry
 
     lax.fori_loop(0, (ndev - 2) // 2, fwd_pair, 0)
-    fwd_act(ndev - 1, p_b, h_b)
-    fwd_out(ndev - 2, h_a)
-    fwd_out(ndev - 1, h_b)
-
-    small(3).wait()
-    small(4).wait()
-    for t in range(tasks):
-        head = hts_in[t].astype(F32)
-        hfs[8 * t:8 * t + ncls, dm * t:dm * (t + 1)] = head
-    hcat[...] = hfs[...].astype(BF16)
-    rows = hfs[:, 0:dm]
-    for t in range(1, tasks):
-        rows = rows + hfs[:, dm * t:dm * (t + 1)]
-    hrow[...] = rows.astype(BF16)
-
-    zs[...] = (xs[...].astype(F32) + zacc[...]).astype(BF16)
-    logits = dot_nt(hrow[...], zs[...])
-    cls = lax.broadcasted_iota(jnp.int32, (8, tok), 0)
-    errs = []
-    for t in range(tasks):
-        lg = jnp.where(cls < ncls, logits[8 * t:8 * t + 8], -jnp.inf)
-        e = jnp.exp(lg - jnp.max(lg, axis=0, keepdims=True))
-        prob = e / jnp.sum(e, axis=0, keepdims=True)
-        errs.append(prob - (cls == labs[t:t + 1, :]).astype(F32))
-    errs.append(jnp.zeros((8, tok), F32))
-    err_t = jnp.concatenate(errs, axis=0).T.astype(BF16)
-    for t in range(tasks):
-        dzs[t] = dot(err_t, hcat[:, dm * t:dm * (t + 1)]).astype(BF16)
+    w2_copy(ndev - 2).wait()
+    w2_copy(ndev - 1).wait()
+    for i in range(2):
+        fwd_out(ndev - 2, h_a, i)
+        fwd_act(ndev - 1, p_b, h_b, 2 * i)
+        fwd_act(ndev - 1, p_b, h_b, 2 * i + 1)
+    cls = lax.broadcasted_iota(jnp.int32, (8, half), 0)
+    zs = []
+    for i in range(2):
+        rows = slice(half * i, half * (i + 1))
+        zs.append((xs[rows].astype(F32) + (zacc[rows] + dot(h_b[rows], w2s[ndev - 1]))).astype(BF16))
+    logits = [dot_nt(hrow[...], z) for z in zs]
+    for i in range(2):
+        rows = slice(half * i, half * (i + 1))
+        errs = []
+        for t in range(tasks):
+            lg = jnp.where(cls < ncls, logits[i][8 * t:8 * t + 8], -jnp.inf)
+            e = jnp.exp(lg - jnp.max(lg, axis=0, keepdims=True))
+            prob = e / jnp.sum(e, axis=0, keepdims=True)
+            errs.append(prob - (cls == labs[t:t + 1, rows]).astype(F32))
+        errs.append(jnp.zeros((8, half), F32))
+        err_t = jnp.concatenate(errs, axis=0).T.astype(BF16)
+        for t in range(tasks):
+            dzs[t, rows] = dot(err_t, hcat[:, dm * t:dm * (t + 1)]).astype(BF16)
 
     pl.semaphore_wait(barrier, ndev - 1)
 
     def blk(s):
-        return lax.rem(me + 1 + s, ndev)
+        flip = ndev - 1 - s
+        b, w = 0, 1
+        while w < ndev:
+            b = b + w * lax.rem(me // w + flip // w, 2)
+            w *= 2
+        return b
 
     def bwd_a(s, dp_ref):
         b = blk(s)
         for t in range(tasks):
             dp_ref[t] = (dot_nt(dzs[t], w2s[b]) * slope[b]).astype(BF16)
 
-    def bwd_b(s, dp_ref):
-        b = blk(s)
-        bm = block_of(bms, b)
+    def bwd_low(s, dp_ref):
+        bm = block_of(bms, blk(s))
+        for t in range(tasks):
+            dlacc[8 * t:8 * t + 8] += dot_nt(bm, dp_ref[t])
+
+    def bwd_col(s, dp_ref):
         for t in range(tasks):
             gbs[s, 8 * t:8 * t + 8] = dot(uts[...], dp_ref[t])
-            dlacc[8 * t:8 * t + 8] += dot_nt(bm, dp_ref[t])
 
     def gb_send(s):
         return pltpu.make_async_remote_copy(src_ref=gbs.at[s], dst_ref=gbr.at[s], send_sem=gb_ss.at[s], recv_sem=gb_rs.at[s],
@@ -166,15 +193,16 @@
         for k in range(2):
             s = 2 * i + k
             bwd_a(s + 1, dps[1 - k])
-            bwd_b(s, dps[k])
-            gb_send(s).start()
+            bwd_low(s, dps[k])
+            bwd_col(s, dps[k])
+        for k in range(2):
+            gb_send(2 * i + k).start()
         return carry
 
     lax.fori_loop(0, (ndev - 2) // 2, bwd_pair, 0)
     bwd_a(ndev - 1, dp_b)
-    bwd_b(ndev - 2, dp_a)
-    gb_send(ndev - 2).start()
-    bwd_b(ndev - 1, dp_b)
+    bwd_low(ndev - 2, dp_a)
+    bwd_low(ndev - 1, dp_b)
 
     ga_t = dot(dlacc[...].astype(BF16), xs[...])
     for k in range(ndev):
@@ -188,11 +216,15 @@
     for off in range(1, ndev):
         ga_send(off).start()
 
+    bwd_col(ndev - 2, dp_a)
+    gb_send(ndev - 2).start()
+    bwd_col(ndev - 1, dp_b)
     gb_sum = gbs[ndev - 1]
     for s in range(ndev - 1):
         gb_send(s).wait_recv()
         gb_sum = gb_sum + gbr[s]
     gb_sum = gb_sum * (1.0 / batch_total)
+    gb_out[...] = gb_sum
 
     pairs = [(t, s) for t in range(tasks) for s in range(t, tasks)]
     gram_b = []
@@ -208,6 +240,7 @@
         ga_send(off).wait_recv()
         ga_sum = ga_sum + gar[off - 1]
     ga_sum = ga_sum * (1.0 / batch_total)
+    ga_out[...] = ga_sum
 
     ms[...] = jnp.zeros_like(ms)
     for p, (t, s) in enumerate(pairs):
@@ -227,22 +260,29 @@
     m_tot = mr[0]
     for k in range(1, ndev):
         m_tot = m_tot + mr[k]
-    m_tot = jnp.sum(m_tot, axis=1, keepdims=True)
-    m_all = jnp.broadcast_to(m_tot, (8, 128))
-
-    gram = {}
-    for p, (t, s) in enumerate(pairs):
-        gram[t, s] = gram[s, t] = jnp.broadcast_to(m_all[p:p + 1, :], (8, 128))
+    m_out[...] = m_tot
+
+    for s in range(ndev - 1):
+        gb_send(s).wait_send()
+    for off in range(1, ndev):
+        ga_send(off).wait_send()
+        m_send(off).wait_send()
+
+
+def solve_kernel(tasks, m_ref, ga_in, gb_in, alpha_ref, ga_ref, gb_ref):
+    m_all = jnp.broadcast_to(jnp.sum(m_ref[...], axis=1, keepdims=True), (8, 128))
+    pairs = [(t, s) for t in range(tasks) for s in range(t, tasks)]
+    gram = {pair: jnp.broadcast_to(m_all[p:p + 1, :], (8, 128)) for p, pair in enumerate(pairs)}
     trace = gram[0, 0]
     for t in range(1, tasks):
         trace = trace + gram[t, t]
     scale = trace / tasks
-    gram = {key: val / scale for key, val in gram.items() if key[0] <= key[1]}
+    gram = {pair: val / scale for pair, val in gram.items()}
 
     def eg_step(_, wts):
         new = []
         for t in range(tasks):
-            acc = gram[min(t, 0), max(t, 0)] * wts[0]
+            acc = gram[0, t] * wts[0]
             for s in range(1, tasks):
                 acc = acc + gram[min(t, s), max(t, s)] * wts[s]
             new.append(wts[t] * jnp.exp(-acc))
@@ -254,27 +294,21 @@
 
     wts = lax.fori_loop(0, EG_STEPS, eg_step, tuple(jnp.full((8, 128), 1.0 / tasks, F32) for _ in range(tasks)))
 
-    ga = wts[0] * ga_sum[0:8]
+    ga = wts[0] * ga_in[0:8]
     for t in range(1, tasks):
-        ga = ga + wts[t] * ga_sum[8 * t:8 * t + 8]
+        ga = ga + wts[t] * ga_in[8 * t:8 * t + 8]
     ga_ref[...] = ga
-    for k in range(fb // 128):
+    for k in range(gb_ref.shape[1] // 128):
         cols = slice(128 * k, 128 * (k + 1))
-        gb = wts[0] * gb_sum[0:8, cols]
+        gb = wts[0] * gb_in[0:8, cols]
         for t in range(1, tasks):
-            gb = gb + wts[t] * gb_sum[8 * t:8 * t + 8, cols]
+            gb = gb + wts[t] * gb_in[8 * t:8 * t + 8, cols]
         gb_ref[:, cols] = gb
     lane = lax.broadcasted_iota(jnp.int32, (8, 128), 1)
     alpha = wts[tasks - 1]
     for t in range(tasks - 1):
         alpha = jnp.where(lane == t, wts[t], alpha)
     alpha_ref[...] = alpha[0:1, 0:tasks]
-
-    for s in range(ndev - 1):
-        gb_send(s).wait_send()
-    for off in range(1, ndev):
-        ga_send(off).wait_send()
-        m_send(off).wait_send()
 
 
 def solution(mesh):
@@ -288,12 +322,12 @@
         own = dm // num_dev
         prow = 8 * tasks + 8
         dma = pltpu.SemaphoreType.DMA
-        hbm = pl.BlockSpec(memory_space=pl.ANY)
+        hbm = pl.BlockSpec(memory_space=pltpu.HBM)
         vmem = pl.BlockSpec(memory_space=pltpu.VMEM)
-        alpha, ga, gb = pl.pallas_call(
+        sums = pl.pallas_call(
             functools.partial(fused_kernel, num_dev, float(tok * num_dev)),
             name="fused_grads",
-            out_shape=(jax.ShapeDtypeStruct((1, tasks), F32), jax.ShapeDtypeStruct((rank, own), F32), jax.ShapeDtypeStruct((rank, fb), F32)),
+            out_shape=(jax.ShapeDtypeStruct((8, 128), F32), jax.ShapeDtypeStruct((8 * tasks, own), F32), jax.ShapeDtypeStruct((8 * tasks, fb), F32)),
             in_specs=[hbm] * 7,
             out_specs=(vmem, vmem, vmem),
             scratch_shapes=[
@@ -312,7 +346,6 @@
                 pltpu.VMEM((tok, fb), BF16),
                 pltpu.VMEM((num_dev, tok, fb), F32),
                 pltpu.VMEM((tok, dm), F32),
-                pltpu.VMEM((tok, dm), BF16),
                 pltpu.VMEM((prow, tasks * dm), F32),
                 pltpu.VMEM((prow, dm), BF16),
                 pltpu.VMEM((prow, tasks * dm), BF16),
@@ -336,8 +369,16 @@
                 dma((num_dev - 1,)),
                 dma((num_dev - 1,)),
             ],
-            compiler_params=pltpu.CompilerParams(collective_id=0, has_side_effects=True, vmem_limit_bytes=60 * 1024 * 1024),
-        )(tokens, labels, w_one, w_two, adapter_a.T, adapter_b, jnp.transpose(task_heads, (0, 2, 1)))
+            compiler_params=pltpu.CompilerParams(collective_id=0, has_side_effects=True, vmem_limit_bytes=48 * 1024 * 1024),
+        )(*[pltpu.with_memory_space_constraint(arr, pltpu.HBM) for arr in (tokens, labels, w_one, w_two, adapter_a.T, adapter_b, jnp.transpose(task_heads, (0, 2, 1)))])
+        alpha, ga, gb = pl.pallas_call(
+            functools.partial(solve_kernel, tasks),
+            name="solve",
+            out_shape=(jax.ShapeDtypeStruct((1, tasks), F32), jax.ShapeDtypeStruct((rank, own), F32), jax.ShapeDtypeStruct((rank, fb), F32)),
+            in_specs=[vmem] * 3,
+            out_specs=(vmem,) * 3,
+            compiler_params=pltpu.CompilerParams(vmem_limit_bytes=2 * 1024 * 1024),
+        )(*sums)
         return alpha.reshape(tasks), ga.T, gb
 
     return jax.shard_map(device_step, mesh=mesh, in_specs=(P("data", None), P(None, "data"), P(), P(), P(), P(), P()), out_specs=(P(), P("data", None), P(None, "data")), check_vma=False)

time: 60 us -> 49.2 us (0.82)
  Pallas kernels: 55.3 us -> 48.5 us
  local copies, waits for them, and re-layouts: 3.76 us -> 0 us
    pallas_call x1, Pallas kernels: 55.3 us -> 47.3 us  [device_step(): pl.pallas_call(functools.partial(fused_kernel, num_dev, float(tok * num_d...]
    unnamed x3 -> x0, local copies, waits for them, and re-layouts: 3.76 us -> none
    pallas_call x0 -> x1, Pallas kernels: none -> 1.16 us  [device_step(): pl.pallas_call(functools.partial(solve_kernel, tasks), name='solve', out_...]
where the time goes in v2:
time: 49.2 us; the launch traced here: 49.1 us
  Pallas kernels  48.5 us (99%)
  between operations  0.64 us (1%)
    pallas_call x1, Pallas kernels, device_step(): pl.pallas_call(functools.partial(fused_kernel, num_dev, float(tok * num_d...  47.3 us
    pallas_call x1, Pallas kernels, device_step(): pl.pallas_call(functools.partial(solve_kernel, tasks), name='solve', out_...  1.16 us

profile of v2, /device:TPU:0, one launch (start us, length us, event | category | flops | bytes accessed | tf_op | source)
XLA Modules:
  0.0 49.1 jit_solution(7210955369428515780)
XLA Ops:
  0.6 47.3 %fused_grads.1 = (f32[8,128]{1,0:T(8,128)S(1)}, f32[24,128]{1,0:T(8,128)S(1)}, f32[24,512]{1,0:T(8,128)S(1)}) custom-call(bf16[512,1024]{1,0:T(8,128)(2,1)} %x_hbm.1, s32[3,512]{1,0:T(4,128)} %lab_hbm.1, bf16[1024,4096]{1,0:T(8,128)(2,1)} %w1_hbm.1, bf16[4096,1024]{1,0:T(8,128)(2,1)} %w2_hbm.1, bf16[8,1024]{1,0:T(8,128)(2,1)} %bitcast.5, ...), custom_call_target="tpu_custom_call" | custom-call | tf_op jit(solution)/shard_map/fused_grads/pallas_call | solution.py:327
  47.9 1.2 %solve.1 = (f32[1,3]{1,0:T(1,128)}, f32[8,128]{1,0:T(8,128)}, f32[8,512]{1,0:T(8,128)}) custom-call(f32[8,128]{1,0:T(8,128)S(1)} %get-tuple-element.9.m_ref, f32[24,128]{1,0:T(8,128)S(1)} %get-tuple-element.10.ga_in, f32[24,512]{1,0:T(8,128)S(1)} %get-tuple-element.11.gb_in), custom_call_target="tpu_custom_call" | custom-call | tf_op jit(solution)/shard_map/solve/pallas_call | solution.py:374

commit v3 on v2

--- a/solution.py
+++ b/solution.py
@@ -27,7 +27,7 @@
 def fused_kernel(ndev, batch_total, x_hbm, lab_hbm, w1_hbm, w2_hbm, at_hbm, bm_hbm, ht_hbm,
                  m_out, ga_out, gb_out,
                  xs, w1s, w2s, ats, bms, hts_in, labs, uts, us, p_a, p_b, h_a, h_b, slope, zacc,
-                 hfs, hrow, hcat, dzs, dp_a, dp_b, dlacc, gbs, gbr, gas, gar, ms, mr,
+                 hrow, hcol, dzs, dp_a, dp_b, dlacc, gbs, gbr, gas, gar, ms, mr,
                  w1sem, w2sem, insem, gb_ss, gb_rs, ga_ss, ga_rs, m_ss, m_rs):
     tok = xs.shape[0]
     dff = w2_hbm.shape[0]
@@ -39,9 +39,14 @@
     own = dm // ndev
     me = lax.axis_index("data")
 
-    barrier = pltpu.get_barrier_semaphore()
-    for off in range(1, ndev):
-        pl.semaphore_signal(barrier, inc=1, device_id=(lax.rem(me + off, ndev),), device_id_type=MESH)
+    def peer_of(flip):
+        b, w = 0, 1
+        while w < ndev:
+            b = b + w * lax.rem(me // w + flip // w, 2)
+            w *= 2
+        return b
+
+    far_first = range(ndev - 1, 0, -1)
 
     def small(i):
         pairs = [(at_hbm, ats), (x_hbm, xs), (bm_hbm, bms), (ht_hbm, hts_in), (lab_hbm, labs)]
@@ -53,7 +58,7 @@
     def w2_copy(j):
         return pltpu.make_async_copy(w2_hbm.at[pl.ds(pl.multiple_of(j * fb, fb), fb), :], w2s.at[j], w2sem.at[j])
 
-    for i in (3, 0, 1):
+    for i in (1, 0, 3):
         small(i).start()
     w1_copy(0).start()
     w1_copy(1).start()
@@ -65,17 +70,20 @@
         w2_copy(j - 1).start()
     w2_copy(ndev - 1).start()
 
+    barrier = pltpu.get_barrier_semaphore()
+    for flip in far_first:
+        pl.semaphore_signal(barrier, inc=1, device_id=(peer_of(flip),), device_id_type=MESH)
+
     zacc[...] = jnp.zeros_like(zacc)
     dlacc[...] = jnp.zeros_like(dlacc)
-    hfs[...] = jnp.zeros_like(hfs)
     small(3).wait()
+    pad = jnp.zeros((8 - ncls, dm), F32)
+    heads = []
     for t in range(tasks):
-        hfs[8 * t:8 * t + ncls, dm * t:dm * (t + 1)] = hts_in[t].astype(F32)
-    hcat[...] = hfs[...].astype(BF16)
-    head_rows = hfs[:, 0:dm]
-    for t in range(1, tasks):
-        head_rows = head_rows + hfs[:, dm * t:dm * (t + 1)]
-    hrow[...] = head_rows.astype(BF16)
+        heads += [hts_in[t].astype(F32), pad]
+    heads = jnp.concatenate(heads + [jnp.zeros((8, dm), F32)], axis=0)
+    hrow[...] = heads.astype(BF16)
+    hcol[...] = heads.T.astype(BF16)
 
     small(0).wait()
     small(1).wait()
@@ -104,11 +112,10 @@
         cdf = 0.5 + 0.5 * t
         h_ref[rows] = (x * cdf).astype(BF16)
         w = cdf * (1.0 - cdf)
-        slope[j, rows] = cdf + x * (w * (2.0 * GELU_C + (6.0 * GELU_C * GELU_A) * x2))
-
-    def fwd_out(j, h_ref, i):
-        rows = slice(half * i, half * (i + 1))
-        zacc[rows] += dot(h_ref[rows], w2s[j])
+        slope[j, :, rows] = (cdf + x * (w * (2.0 * GELU_C + (6.0 * GELU_C * GELU_A) * x2))).T
+
+    def fwd_out(j, h_ref):
+        zacc[...] += dot(h_ref[...], w2s[j])
 
     ps, hs = (p_a, p_b), (h_a, h_b)
     for i in range(2):
@@ -127,81 +134,91 @@
             for q in range(4):
                 if q < 2:
                     fwd_in(j + 2, ps[k], q)
-                else:
-                    fwd_out(j, hs[k], q - 2)
+                elif q == 2:
+                    fwd_out(j, hs[k])
                 fwd_act(j + 1, ps[1 - k], hs[1 - k], q)
         return carry
 
     lax.fori_loop(0, (ndev - 2) // 2, fwd_pair, 0)
+    pl.semaphore_wait(barrier, ndev - 1)
     w2_copy(ndev - 2).wait()
     w2_copy(ndev - 1).wait()
+    fwd_out(ndev - 2, h_a)
     for i in range(2):
-        fwd_out(ndev - 2, h_a, i)
         fwd_act(ndev - 1, p_b, h_b, 2 * i)
         fwd_act(ndev - 1, p_b, h_b, 2 * i + 1)
     cls = lax.broadcasted_iota(jnp.int32, (8, half), 0)
-    zs = []
+    z = (xs[...].astype(F32) + (zacc[...] + dot(h_b[...], w2s[ndev - 1]))).astype(BF16)
+    both = dot_nt(hrow[...], z)
+    logits = [both[:, :half], both[:, half:]]
+    errs = [[] for _ in range(tasks)]
     for i in range(2):
         rows = slice(half * i, half * (i + 1))
-        zs.append((xs[rows].astype(F32) + (zacc[rows] + dot(h_b[rows], w2s[ndev - 1]))).astype(BF16))
-    logits = [dot_nt(hrow[...], z) for z in zs]
-    for i in range(2):
-        rows = slice(half * i, half * (i + 1))
-        errs = []
         for t in range(tasks):
             lg = jnp.where(cls < ncls, logits[i][8 * t:8 * t + 8], -jnp.inf)
             e = jnp.exp(lg - jnp.max(lg, axis=0, keepdims=True))
             prob = e / jnp.sum(e, axis=0, keepdims=True)
-            errs.append(prob - (cls == labs[t:t + 1, rows]).astype(F32))
-        errs.append(jnp.zeros((8, half), F32))
-        err_t = jnp.concatenate(errs, axis=0).T.astype(BF16)
-        for t in range(tasks):
-            dzs[t, rows] = dot(err_t, hcat[:, dm * t:dm * (t + 1)]).astype(BF16)
-
-    pl.semaphore_wait(barrier, ndev - 1)
+            errs[t].append(prob - (cls == labs[t:t + 1, rows]).astype(F32))
+    blank = jnp.zeros((8, tok), F32)
+    for t in range(tasks):
+        err = jnp.concatenate([jnp.concatenate(errs[t], axis=1) if k == t else blank for k in range(tasks + 1)], axis=0)
+        dzs[t] = dot(hcol[...], err.astype(BF16)).astype(BF16)
+
 
     def blk(s):
-        flip = ndev - 1 - s
-        b, w = 0, 1
-        while w < ndev:
-            b = b + w * lax.rem(me // w + flip // w, 2)
-            w *= 2
-        return b
-
-    def bwd_a(s, dp_ref):
+        return peer_of(ndev - 1 - s)
+
+    def low_piece(s, dp_ref, t, i):
+        part = slice(fb // 2 * i, fb // 2 * (i + 1))
+        return dot(block_of(bms, blk(s))[:, part], dp_ref[t, part, :])
+
+    def col_piece(dp_ref, t, i):
+        part = slice(tok // 2 * i, tok // 2 * (i + 1))
+        return dot_nt(uts[:, part], dp_ref[t, :, part])
+
+    def bwd_step(s, dp_new, dp_old, cols=True):
         b = blk(s)
         for t in range(tasks):
-            dp_ref[t] = (dot_nt(dzs[t], w2s[b]) * slope[b]).astype(BF16)
+            dh, low, col = None, [], []
+            for q in range(4):
+                part = slice(dm // 4 * q, dm // 4 * (q + 1))
+                piece = dot(w2s[b, :, part], dzs[t, part, :])
+                dh = piece if dh is None else dh + piece
+                if dp_old is not None:
+                    if q % 2 == 0 and cols:
+                        col.append(col_piece(dp_old, t, q // 2))
+                    if q % 2 == 1:
+                        low.append(low_piece(s - 1, dp_old, t, q // 2))
+            dp_new[t] = (dh * slope[b]).astype(BF16)
+            if low:
+                dlacc[8 * t:8 * t + 8] += low[0] + low[1]
+            if col:
+                gbs[s - 1, 8 * t:8 * t + 8] = col[0] + col[1]
 
     def bwd_low(s, dp_ref):
-        bm = block_of(bms, blk(s))
         for t in range(tasks):
-            dlacc[8 * t:8 * t + 8] += dot_nt(bm, dp_ref[t])
+            dlacc[8 * t:8 * t + 8] += low_piece(s, dp_ref, t, 0) + low_piece(s, dp_ref, t, 1)
 
     def bwd_col(s, dp_ref):
         for t in range(tasks):
-            gbs[s, 8 * t:8 * t + 8] = dot(uts[...], dp_ref[t])
+            gbs[s, 8 * t:8 * t + 8] = col_piece(dp_ref, t, 0) + col_piece(dp_ref, t, 1)
 
     def gb_send(s):
         return pltpu.make_async_remote_copy(src_ref=gbs.at[s], dst_ref=gbr.at[s], send_sem=gb_ss.at[s], recv_sem=gb_rs.at[s],
                                             device_id=(blk(s),), device_id_type=MESH)
 
     dps = (dp_a, dp_b)
-    bwd_a(0, dp_a)
+    bwd_step(0, dp_a, None)
 
     def bwd_pair(i, carry):
         for k in range(2):
-            s = 2 * i + k
-            bwd_a(s + 1, dps[1 - k])
-            bwd_low(s, dps[k])
-            bwd_col(s, dps[k])
+            bwd_step(2 * i + k + 1, dps[1 - k], dps[k])
         for k in range(2):
             gb_send(2 * i + k).start()
         return carry
 
     lax.fori_loop(0, (ndev - 2) // 2, bwd_pair, 0)
-    bwd_a(ndev - 1, dp_b)
-    bwd_low(ndev - 2, dp_a)
+    bwd_step(ndev - 1, dp_b, dp_a, cols=False)
     bwd_low(ndev - 1, dp_b)
 
     ga_t = dot(dlacc[...].astype(BF16), xs[...])
@@ -209,11 +226,11 @@
         gas[k] = ga_t[:8 * tasks, own * k:own * (k + 1)]
 
     def ga_send(off):
-        peer = lax.rem(me + off, ndev)
+        peer = peer_of(off)
         return pltpu.make_async_remote_copy(src_ref=gas.at[peer], dst_ref=gar.at[off - 1], send_sem=ga_ss.at[off - 1], recv_sem=ga_rs.at[off - 1],
                                             device_id=(peer,), device_id_type=MESH)
 
-    for off in range(1, ndev):
+    for off in far_first:
         ga_send(off).start()
 
     bwd_col(ndev - 2, dp_a)
@@ -242,17 +259,22 @@
     ga_sum = ga_sum * (1.0 / batch_total)
     ga_out[...] = ga_sum
 
-    ms[...] = jnp.zeros_like(ms)
+    rows = []
     for p, (t, s) in enumerate(pairs):
         prod = ga_sum[8 * t:8 * t + 8] * ga_sum[8 * s:8 * s + 8] + gram_b[p]
-        ms[p:p + 1, :] = jnp.sum(prod, axis=0, keepdims=True)
+        rows.append(jnp.sum(prod, axis=0, keepdims=True))
+    lane = lax.broadcasted_iota(jnp.int32, (1, 128), 1)
+    m_own = jnp.zeros((1, 128), F32)
+    for p, row in enumerate(rows):
+        m_own = jnp.where(lane == p, jnp.sum(row, axis=1, keepdims=True), m_own)
+    ms[...] = m_own
 
     def m_send(off):
-        peer = lax.rem(me + off, ndev)
+        peer = peer_of(off)
         return pltpu.make_async_remote_copy(src_ref=ms, dst_ref=mr.at[me], send_sem=m_ss.at[off - 1], recv_sem=m_rs.at[off - 1],
                                             device_id=(peer,), device_id_type=MESH)
 
-    for off in range(1, ndev):
+    for off in far_first:
         m_send(off).start()
     mr[me] = ms[...]
     for off in range(1, ndev):
@@ -270,9 +292,9 @@
 
 
 def solve_kernel(tasks, m_ref, ga_in, gb_in, alpha_ref, ga_ref, gb_ref):
-    m_all = jnp.broadcast_to(jnp.sum(m_ref[...], axis=1, keepdims=True), (8, 128))
+    m_all = m_ref[...]
     pairs = [(t, s) for t in range(tasks) for s in range(t, tasks)]
-    gram = {pair: jnp.broadcast_to(m_all[p:p + 1, :], (8, 128)) for p, pair in enumerate(pairs)}
+    gram = {pair: jnp.broadcast_to(m_all[:, p:p + 1], (8, 128)) for p, pair in enumerate(pairs)}
     trace = gram[0, 0]
     for t in range(1, tasks):
         trace = trace + gram[t, t]
@@ -292,7 +314,7 @@
         inv = 1.0 / tot
         return tuple(w * inv for w in new)
 
-    wts = lax.fori_loop(0, EG_STEPS, eg_step, tuple(jnp.full((8, 128), 1.0 / tasks, F32) for _ in range(tasks)))
+    wts = lax.fori_loop(0, EG_STEPS, eg_step, tuple(jnp.full((8, 128), 1.0 / tasks, F32) for _ in range(tasks)), unroll=5)
 
     ga = wts[0] * ga_in[0:8]
     for t in range(1, tasks):
@@ -327,7 +349,7 @@
         sums = pl.pallas_call(
             functools.partial(fused_kernel, num_dev, float(tok * num_dev)),
             name="fused_grads",
-            out_shape=(jax.ShapeDtypeStruct((8, 128), F32), jax.ShapeDtypeStruct((8 * tasks, own), F32), jax.ShapeDtypeStruct((8 * tasks, fb), F32)),
+            out_shape=(jax.ShapeDtypeStruct((1, 128), F32), jax.ShapeDtypeStruct((8 * tasks, own), F32), jax.ShapeDtypeStruct((8 * tasks, fb), F32)),
             in_specs=[hbm] * 7,
             out_specs=(vmem, vmem, vmem),
             scratch_shapes=[
@@ -344,21 +366,20 @@
                 pltpu.VMEM((tok, fb), F32),
                 pltpu.VMEM((tok, fb), BF16),
                 pltpu.VMEM((tok, fb), BF16),
-                pltpu.VMEM((num_dev, tok, fb), F32),
+                pltpu.VMEM((num_dev, fb, tok), F32),
                 pltpu.VMEM((tok, dm), F32),
-                pltpu.VMEM((prow, tasks * dm), F32),
                 pltpu.VMEM((prow, dm), BF16),
-                pltpu.VMEM((prow, tasks * dm), BF16),
-                pltpu.VMEM((tasks, tok, dm), BF16),
-                pltpu.VMEM((tasks, tok, fb), BF16),
-                pltpu.VMEM((tasks, tok, fb), BF16),
+                pltpu.VMEM((dm, prow), BF16),
+                pltpu.VMEM((tasks, dm, tok), BF16),
+                pltpu.VMEM((tasks, fb, tok), BF16),
+                pltpu.VMEM((tasks, fb, tok), BF16),
                 pltpu.VMEM((prow, tok), F32),
                 pltpu.VMEM((num_dev, 8 * tasks, fb), F32),
                 pltpu.VMEM((num_dev - 1, 8 * tasks, fb), F32),
                 pltpu.VMEM((num_dev, 8 * tasks, own), F32),
                 pltpu.VMEM((num_dev - 1, 8 * tasks, own), F32),
-                pltpu.VMEM((8, 128), F32),
-                pltpu.VMEM((num_dev, 8, 128), F32),
+                pltpu.VMEM((1, 128), F32),
+                pltpu.VMEM((num_dev, 1, 128), F32),
                 dma((num_dev,)),
                 dma((num_dev,)),
                 dma((5,)),

time: 49.2 us -> 48.1 us (0.978)
  Pallas kernels: 48.5 us -> 47.4 us
    pallas_call x1, Pallas kernels: 47.3 us -> 46.3 us  [device_step(): pl.pallas_call(functools.partial(fused_kernel, num_dev, float(tok * num_d...]
where the time goes in v3:
time: 48.1 us; the launch traced here: 48 us
  Pallas kernels  47.4 us (99%)
  between operations  0.64 us (1%)
    pallas_call x1, Pallas kernels, device_step(): pl.pallas_call(functools.partial(fused_kernel, num_dev, float(tok * num_d...  46.3 us
    pallas_call x1, Pallas kernels, device_step(): pl.pallas_call(functools.partial(solve_kernel, tasks), name='solve', out_...  1.13 us

profile of v3, /device:TPU:0, one launch (start us, length us, event | category | flops | bytes accessed | tf_op | source)
XLA Modules:
  0.0 48.0 jit_solution(10735873626859510243)
XLA Ops:
  0.6 46.3 %fused_grads.1 = (f32[1,128]{1,0:T(1,128)S(1)}, f32[24,128]{1,0:T(8,128)S(1)}, f32[24,512]{1,0:T(8,128)S(1)}) custom-call(bf16[512,1024]{1,0:T(8,128)(2,1)} %x_hbm.1, s32[3,512]{1,0:T(4,128)} %lab_hbm.1, bf16[1024,4096]{1,0:T(8,128)(2,1)} %w1_hbm.1, bf16[4096,1024]{1,0:T(8,128)(2,1)} %w2_hbm.1, bf16[8,1024]{1,0:T(8,128)(2,1)} %bitcast.5, ...), custom_call_target="tpu_custom_call" | custom-call | tf_op jit(solution)/shard_map/fused_grads/pallas_call | solution.py:349
  46.9 1.1 %solve.1 = (f32[1,3]{1,0:T(1,128)}, f32[8,128]{1,0:T(8,128)}, f32[8,512]{1,0:T(8,128)}) custom-call(f32[1,128]{1,0:T(1,128)S(1)} %get-tuple-element.9.m_ref, f32[24,128]{1,0:T(8,128)S(1)} %get-tuple-element.10.ga_in, f32[24,512]{1,0:T(8,128)S(1)} %get-tuple-element.11.gb_in), custom_call_target="tpu_custom_call" | custom-call | tf_op jit(solution)/shard_map/solve/pallas_call | solution.py:395

commit v4 on v3

--- a/solution.py
+++ b/solution.py
@@ -26,7 +26,7 @@
 
 def fused_kernel(ndev, batch_total, x_hbm, lab_hbm, w1_hbm, w2_hbm, at_hbm, bm_hbm, ht_hbm,
                  m_out, ga_out, gb_out,
-                 xs, w1s, w2s, ats, bms, hts_in, labs, uts, us, p_a, p_b, h_a, h_b, slope, zacc,
+                 xs, w1s, w2s, ats, bms, hts_in, labs, uts, us, p_a, p_b, h_a, h_b, h_c, slope, zacc,
                  hrow, hcol, dzs, dp_a, dp_b, dlacc, gbs, gbr, gas, gar, ms, mr,
                  w1sem, w2sem, insem, gb_ss, gb_rs, ga_ss, ga_rs, m_ss, m_rs):
     tok = xs.shape[0]
@@ -117,7 +117,7 @@
     def fwd_out(j, h_ref):
         zacc[...] += dot(h_ref[...], w2s[j])
 
-    ps, hs = (p_a, p_b), (h_a, h_b)
+    ps, hs = (p_a, p_b), (h_a, h_b, h_c)
     for i in range(2):
         fwd_in(0, p_a, i)
     for i in range(2):
@@ -134,9 +134,9 @@
             for q in range(4):
                 if q < 2:
                     fwd_in(j + 2, ps[k], q)
-                elif q == 2:
-                    fwd_out(j, hs[k])
-                fwd_act(j + 1, ps[1 - k], hs[1 - k], q)
+                fwd_act(j + 1, ps[1 - k], hs[1 + k], q)
+        zacc[...] += dot(h_a[...], w2s[2 * i]) + dot(h_b[...], w2s[2 * i + 1])
+        h_a[...] = h_c[...]
         return carry
 
     lax.fori_loop(0, (ndev - 2) // 2, fwd_pair, 0)
@@ -184,11 +184,10 @@
                 part = slice(dm // 4 * q, dm // 4 * (q + 1))
                 piece = dot(w2s[b, :, part], dzs[t, part, :])
                 dh = piece if dh is None else dh + piece
-                if dp_old is not None:
-                    if q % 2 == 0 and cols:
+                if dp_old is not None and q % 2 == 0:
+                    if cols:
                         col.append(col_piece(dp_old, t, q // 2))
-                    if q % 2 == 1:
-                        low.append(low_piece(s - 1, dp_old, t, q // 2))
+                    low.append(low_piece(s - 1, dp_old, t, q // 2))
             dp_new[t] = (dh * slope[b]).astype(BF16)
             if low:
                 dlacc[8 * t:8 * t + 8] += low[0] + low[1]
@@ -366,6 +365,7 @@
                 pltpu.VMEM((tok, fb), F32),
                 pltpu.VMEM((tok, fb), BF16),
                 pltpu.VMEM((tok, fb), BF16),
+                pltpu.VMEM((tok, fb), BF16),
                 pltpu.VMEM((num_dev, fb, tok), F32),
                 pltpu.VMEM((tok, dm), F32),
                 pltpu.VMEM((prow, dm), BF16),

time: 48.1 us -> 48.1 us (level)
  no operation moved by 1% of the time
where the time goes in v4:
time: 48.1 us; the launch traced here: 48 us
  Pallas kernels  47.4 us (99%)
  between operations  0.64 us (1%)
    pallas_call x1, Pallas kernels, device_step(): pl.pallas_call(functools.partial(fused_kernel, num_dev, float(tok * num_d...  46.3 us
    pallas_call x1, Pallas kernels, device_step(): pl.pallas_call(functools.partial(solve_kernel, tasks), name='solve', out_...  1.13 us

profile of v4, /device:TPU:0, one launch (start us, length us, event | category | flops | bytes accessed | tf_op | source)
XLA Modules:
  0.0 48.0 jit_solution(4725918485309990162)
XLA Ops:
  0.6 46.3 %fused_grads.1 = (f32[1,128]{1,0:T(1,128)S(1)}, f32[24,128]{1,0:T(8,128)S(1)}, f32[24,512]{1,0:T(8,128)S(1)}) custom-call(bf16[512,1024]{1,0:T(8,128)(2,1)} %x_hbm.1, s32[3,512]{1,0:T(4,128)} %lab_hbm.1, bf16[1024,4096]{1,0:T(8,128)(2,1)} %w1_hbm.1, bf16[4096,1024]{1,0:T(8,128)(2,1)} %w2_hbm.1, bf16[8,1024]{1,0:T(8,128)(2,1)} %bitcast.5, ...), custom_call_target="tpu_custom_call" | custom-call | tf_op jit(solution)/shard_map/fused_grads/pallas_call | solution.py:348
  46.9 1.1 %solve.1 = (f32[1,3]{1,0:T(1,128)}, f32[8,128]{1,0:T(8,128)}, f32[8,512]{1,0:T(8,128)}) custom-call(f32[1,128]{1,0:T(1,128)S(1)} %get-tuple-element.9.m_ref, f32[24,128]{1,0:T(8,128)S(1)} %get-tuple-element.10.ga_in, f32[24,512]{1,0:T(8,128)S(1)} %get-tuple-element.11.gb_in), custom_call_target="tpu_custom_call" | custom-call | tf_op jit(solution)/shard_map/solve/pallas_call | solution.py:395

commit v5 on v4

--- a/solution.py
+++ b/solution.py
@@ -313,7 +313,7 @@
         inv = 1.0 / tot
         return tuple(w * inv for w in new)
 
-    wts = lax.fori_loop(0, EG_STEPS, eg_step, tuple(jnp.full((8, 128), 1.0 / tasks, F32) for _ in range(tasks)), unroll=5)
+    wts = lax.fori_loop(0, EG_STEPS, eg_step, tuple(jnp.full((8, 128), 1.0 / tasks, F32) for _ in range(tasks)), unroll=EG_STEPS)
 
     ga = wts[0] * ga_in[0:8]
     for t in range(1, tasks):

time: 48.1 us -> 48.1 us (level)
  no operation moved by 1% of the time
where the time goes in v5:
time: 48.1 us; the launch traced here: 48 us
  Pallas kernels  47.4 us (99%)
  between operations  0.64 us (1%)
    pallas_call x1, Pallas kernels, device_step(): pl.pallas_call(functools.partial(fused_kernel, num_dev, float(tok * num_d...  46.3 us
    pallas_call x1, Pallas kernels, device_step(): pl.pallas_call(functools.partial(solve_kernel, tasks), name='solve', out_...  1.13 us

profile of v5, /device:TPU:0, one launch (start us, length us, event | category | flops | bytes accessed | tf_op | source)
XLA Modules:
  0.0 48.0 jit_solution(2348607176885966936)
XLA Ops:
  0.6 46.3 %fused_grads.1 = (f32[1,128]{1,0:T(1,128)S(1)}, f32[24,128]{1,0:T(8,128)S(1)}, f32[24,512]{1,0:T(8,128)S(1)}) custom-call(bf16[512,1024]{1,0:T(8,128)(2,1)} %x_hbm.1, s32[3,512]{1,0:T(4,128)} %lab_hbm.1, bf16[1024,4096]{1,0:T(8,128)(2,1)} %w1_hbm.1, bf16[4096,1024]{1,0:T(8,128)(2,1)} %w2_hbm.1, bf16[8,1024]{1,0:T(8,128)(2,1)} %bitcast.5, ...), custom_call_target="tpu_custom_call" | custom-call | tf_op jit(solution)/shard_map/fused_grads/pallas_call | solution.py:348
  46.9 1.1 %solve.1 = (f32[1,3]{1,0:T(1,128)}, f32[8,128]{1,0:T(8,128)}, f32[8,512]{1,0:T(8,128)}) custom-call(f32[1,128]{1,0:T(1,128)S(1)} %get-tuple-element.9.m_ref, f32[24,128]{1,0:T(8,128)S(1)} %get-tuple-element.10.ga_in, f32[24,512]{1,0:T(8,128)S(1)} %get-tuple-element.11.gb_in), custom_call_target="tpu_custom_call" | custom-call | tf_op jit(solution)/shard_map/solve/pallas_call | solution.py:395
